TPU v7x, 256 devices: a whole 4x4x8 slice. The times are simulated.
256 devices in a mesh: walk: 32 (over z, x), chol: 8 (over y, core).
Axes of the slice: x: 4, y: 4, z: 8, core: 2. Of those that a mesh axis runs over, the one named last changes fastest.
Arguments:
- orbitals: bfloat16 [32, 400, 2048], P('walk', None, 'chol'), may hold values from -4 to 4
- intersection_inv: bfloat16 [32, 400, 400], P('walk'), may hold values from -0.18 to 0.18
- interp: bfloat16 [2048, 4096], P(None, 'chol'), may hold values from -0.079549513 to 0.079549513
- occ_interp: bfloat16 [400, 4096], P(None, 'chol'), may hold values from -0.18 to 0.18
- chol_factors: bfloat16 [4096, 8192], P('chol', 'walk'), may hold values from -2 to 2
- fields: float32 [32, 8192], P(None, 'walk'), may hold values from -4 to 4
Outputs:
- new_orbitals: bfloat16 [32, 400, 2048], P('walk', None, 'chol')
- force_bias: float32 [32, 8192], P(None, 'walk')
All inputs are finite; a program needn't handle non-finite values.
Results may differ from a plain program's by a relative error of at most 0.017.
Values may be sent and summed in bfloat16 or wider, within the bound.
A program may use at most 64 MiB of HBM per device.

v0:
```python
import jax
import jax.numpy as jnp
from jax import lax
from jax.sharding import PartitionSpec as P

TERMS = 4


time_root = 2.2


def joined_along(blocks, dim):
    blocks = jnp.moveaxis(blocks, 0, dim)
    dims = blocks.shape
    return blocks.reshape(*dims[:dim], dims[dim] * dims[dim + 1], *dims[dim + 2 :])


def sent_to_all(value, axis):
    length = lax.axis_size(axis)
    return lax.all_to_all(
        jnp.broadcast_to(value[None], (length, *value.shape)), axis, 0, 0, tiled=True
    )


def collect(value, axis, dim):
    return joined_along(sent_to_all(value, axis), dim)


def of_everyone(value, axis):
    everything = sent_to_all(value, axis)
    return jnp.sum(everything, axis=0)


def cut_along(value, dim, length):
    dims = value.shape
    blocks = value.reshape(*dims[:dim], length, dims[dim] // length, *dims[dim + 1 :])
    return jnp.moveaxis(blocks, dim, 0)


def sum_at_owner(value, axis, dim):
    length = lax.axis_size(axis)
    blocks = lax.all_to_all(cut_along(value, dim, length), axis, 0, 0, tiled=True)
    return jnp.sum(blocks, axis=0)


def sent_and_summed(value, axis, dim):
    blocks = cut_along(value, dim, lax.axis_size(axis))
    arrived = lax.all_to_all(blocks, axis, split_axis=0, concat_axis=0, tiled=True)
    return arrived.astype(jnp.float32).sum(axis=0)


def on_device(orbitals, intersection_inv, interp, occ_interp, chol_factors, fields):
    piece = collect(orbitals, "chol", 2)
    green = jnp.einsum(
        "wij,wjm->wim", intersection_inv, piece, preferred_element_type=jnp.float32
    ).astype(jnp.bfloat16)
    projected = jnp.einsum("wim,mp->wip", green, interp, preferred_element_type=jnp.float32)
    applied = jnp.einsum("wim,mp->wip", piece, interp, preferred_element_type=jnp.float32)
    projected, current = (projected, applied)
    weights = jnp.sum(occ_interp.astype(jnp.float32)[None] * projected, axis=1)
    factors = chol_factors.astype(jnp.float32)
    all_weights = collect(weights, "walk", 0)
    partial_bias = jnp.dot(all_weights, factors, precision=lax.Precision.HIGHEST)
    force_bias = of_everyone(partial_bias, "chol")
    coeff = time_root * (fields - force_bias)
    field_part = jnp.dot(coeff, factors.T, precision=lax.Precision.HIGHEST)
    scales = sum_at_owner(field_part, "walk", 0)
    total = orbitals.astype(jnp.float32)
    for order in range(1, TERMS + 1):
        mixed = (current * scales[:, None, :] / order).astype(jnp.bfloat16)
        partial_value = jnp.einsum("wnp,mp->wnm", mixed, interp, preferred_element_type=jnp.float32)
        term_local = sent_and_summed(partial_value.astype(jnp.bfloat16), "chol", 2).astype(
            jnp.bfloat16
        )
        total = total + term_local.astype(jnp.float32)
        if order < TERMS:
            current = jnp.einsum(
                "wim,mp->wip",
                collect(term_local, "chol", 2),
                interp,
                preferred_element_type=jnp.float32,
            )
    return (total.astype(jnp.bfloat16), force_bias)


def solution(mesh):
    placed = (
        P("walk", None, "chol"),
        P("walk", None, None),
        P(None, "chol"),
        P(None, "chol"),
        P("chol", "walk"),
        P(None, "walk"),
    )
    return jax.shard_map(
        on_device,
        mesh=mesh,
        in_specs=placed,
        out_specs=(P("walk", None, "chol"), P(None, "walk")),
        check_vma=False,
    )
```

profile of v0, /device:TPU:1, one launch (start us, length us, event | category | flops | bytes accessed | tf_op | source)
XLA Modules:
  0.0 294.1 jit_solution(12566781795822847072)
XLA Ops:
  0.6 1.2 broadcast_in_dim.15
  1.8 27.3 %all_to_all.55 = bf16[8,1,400,256]{3,2,1,0:T(8,128)(2,1)S(1)} all-to-all(bf16[8,1,400,256]{3,2,1,0:T(8,128)(2,1)S(1)} %broadcast_in_dim.15), channel_id=1, replica_groups=mesh['walk'=32,'chol'=8] {'chol'}, dimensions={0} | all-to-all | bytes 3276800 | tf_op jit(solution)/shard_map/all_to_all | solution.py:20
  29.1 1.4 copy.27
  30.6 3.4 %fusion.7 = f32[512]{0:T(512)S(1)} fusion(bf16[2048,512]{1,0:T(8,128)(2,1)S(1)} %copy-done, bf16[400,2048]{1,0:T(8,128)(2,1)} %bitcast.98, bf16[400,512]{1,0:T(8,128)(2,1)S(1)} %copy-done.5, bf16[1,400,400]{2,1,0:T(8,128)(2,1)S(1)} %copy-done.6), kind=kOutput, calls=%fused_computation.21 | convolution fusion | flops 1495653888 | bytes 4467200 | tf_op jit(solution)/shard_map/wim,mp->wip/dot_general | solution.py:57
  34.0 19.7 %all_to_all.56 = f32[32,1,512]{2,1,0:T(1,128)S(1)} all-to-all(f32[32,1,512]{2,1,0:T(1,128)S(1)} %broadcast_in_dim.16), channel_id=1, replica_groups=mesh['walk'=32,'chol'=8] {'walk'}, dimensions={0} | all-to-all | bytes 131072 | tf_op jit(solution)/shard_map/all_to_all | solution.py:20
  53.9 11.1 %all_to_all.57 = f32[8,32,256]{2,1,0:T(8,128)S(1)} all-to-all(f32[8,32,256]{2,1,0:T(8,128)S(1)} %broadcast_in_dim.17), channel_id=1, replica_groups=mesh['walk'=32,'chol'=8] {'chol'}, dimensions={0} | all-to-all | bytes 524288 | tf_op jit(solution)/shard_map/all_to_all | solution.py:20
  65.4 11.8 %all_to_all.58 = f32[32,1,512]{2,1,0:T(1,128)S(1)} all-to-all(f32[32,1,512]{2,1,0:T(1,128)S(1)} %copy.18), channel_id=1, replica_groups=mesh['walk'=32,'chol'=8] {'walk'}, dimensions={0} | all-to-all | bytes 131072 | tf_op jit(solution)/shard_map/all_to_all | solution.py:42
  77.3 4.5 %convolution_convert_fusion.3 = bf16[400,2048]{1,0:T(8,128)(2,1)} fusion(bf16[2048,512]{1,0:T(8,128)(2,1)S(1)} %copy-done, bf16[400,2048]{1,0:T(8,128)(2,1)} %bitcast.99, f32[512]{0:T(512)S(1)} %reduce_sum.77), kind=kOutput, calls=%fused_computation.3 | convolution fusion | flops 1678950400 | bytes 5376000 | tf_op jit(solution)/shard_map/wnp,mp->wnm/dot_general | solution.py:71
  81.8 1.9 copy.28
  83.8 0.3 copy.50
  84.1 27.0 %all_to_all.59 = bf16[8,1,400,256]{3,2,1,0:T(8,128)(2,1)} all-to-all(bf16[8,1,400,256]{3,2,1,0:T(8,128)(2,1)S(1)} %bitcast.88), channel_id=1, replica_groups=mesh['walk'=32,'chol'=8] {'chol'}, dimensions={0} | all-to-all | bytes 3276800 | tf_op jit(solution)/shard_map/all_to_all | solution.py:48
  111.1 1.7 reduce_sum.78
  112.9 24.7 %all_to_all.60 = bf16[8,1,400,256]{3,2,1,0:T(8,128)(2,1)S(1)} all-to-all(bf16[8,1,400,256]{3,2,1,0:T(8,128)(2,1)S(1)} %broadcast_in_dim.18), channel_id=1, replica_groups=mesh['walk'=32,'chol'=8] {'chol'}, dimensions={0} | all-to-all | bytes 3276800 | tf_op jit(solution)/shard_map/all_to_all | solution.py:20
  137.6 1.4 copy.29
  139.0 4.5 %convolution_convert_fusion.2 = bf16[400,2048]{1,0:T(8,128)(2,1)} fusion(bf16[2048,512]{1,0:T(8,128)(2,1)S(1)} %copy-done, bf16[400,2048]{1,0:T(8,128)(2,1)} %bitcast.103, f32[512]{0:T(512)S(1)} %reduce_sum.77), kind=kOutput, calls=%fused_computation.2 | convolution fusion | flops 1679155200 | bytes 5376000 | tf_op jit(solution)/shard_map/wnp,mp->wnm/dot_general | solution.py:71
  143.5 1.9 copy.30
  145.4 0.3 copy.49
  145.8 25.4 %all_to_all.61 = bf16[8,1,400,256]{3,2,1,0:T(8,128)(2,1)} all-to-all(bf16[8,1,400,256]{3,2,1,0:T(8,128)(2,1)S(1)} %bitcast.91), channel_id=1, replica_groups=mesh['walk'=32,'chol'=8] {'chol'}, dimensions={0} | all-to-all | bytes 3276800 | tf_op jit(solution)/shard_map/all_to_all | solution.py:48
  171.2 1.7 reduce_sum.79
  173.0 24.7 %all_to_all.62 = bf16[8,1,400,256]{3,2,1,0:T(8,128)(2,1)S(1)} all-to-all(bf16[8,1,400,256]{3,2,1,0:T(8,128)(2,1)S(1)} %broadcast_in_dim.19), channel_id=1, replica_groups=mesh['walk'=32,'chol'=8] {'chol'}, dimensions={0} | all-to-all | bytes 3276800 | tf_op jit(solution)/shard_map/all_to_all | solution.py:20
  197.7 1.4 copy.31
  199.1 4.5 %convolution_convert_fusion.1 = bf16[400,2048]{1,0:T(8,128)(2,1)} fusion(bf16[2048,512]{1,0:T(8,128)(2,1)S(1)} %copy-done, bf16[400,2048]{1,0:T(8,128)(2,1)} %bitcast.105, f32[512]{0:T(512)S(1)} %reduce_sum.77), kind=kOutput, calls=%fused_computation.1 | convolution fusion | flops 1679155200 | bytes 5376000 | tf_op jit(solution)/shard_map/wnp,mp->wnm/dot_general | solution.py:71
  203.6 1.9 copy.32
  205.9 25.4 %all_to_all.63 = bf16[8,1,400,256]{3,2,1,0:T(8,128)(2,1)} all-to-all(bf16[8,1,400,256]{3,2,1,0:T(8,128)(2,1)S(1)} %bitcast.94), channel_id=1, replica_groups=mesh['walk'=32,'chol'=8] {'chol'}, dimensions={0} | all-to-all | bytes 3276800 | tf_op jit(solution)/shard_map/all_to_all | solution.py:48
  231.3 1.7 reduce_sum.80
  233.2 24.7 %all_to_all.64 = bf16[8,1,400,256]{3,2,1,0:T(8,128)(2,1)S(1)} all-to-all(bf16[8,1,400,256]{3,2,1,0:T(8,128)(2,1)S(1)} %broadcast_in_dim.20), channel_id=1, replica_groups=mesh['walk'=32,'chol'=8] {'chol'}, dimensions={0} | all-to-all | bytes 3276800 | tf_op jit(solution)/shard_map/all_to_all | solution.py:20
  257.9 1.4 copy.33
  259.3 4.5 %convolution_convert_fusion = bf16[400,2048]{1,0:T(8,128)(2,1)} fusion(bf16[2048,512]{1,0:T(8,128)(2,1)S(1)} %copy-done, bf16[400,2048]{1,0:T(8,128)(2,1)} %bitcast.100, f32[512]{0:T(512)S(1)} %reduce_sum.77), kind=kOutput, calls=%fused_computation | convolution fusion | flops 1679155200 | bytes 5376000 | tf_op jit(solution)/shard_map/wnp,mp->wnm/dot_general | solution.py:71
  263.8 1.9 copy.34
  266.0 25.4 %all_to_all.65 = bf16[8,1,400,256]{3,2,1,0:T(8,128)(2,1)} all-to-all(bf16[8,1,400,256]{3,2,1,0:T(8,128)(2,1)S(1)} %bitcast.97), channel_id=1, replica_groups=mesh['walk'=32,'chol'=8] {'chol'}, dimensions={0} | all-to-all | bytes 3276800 | tf_op jit(solution)/shard_map/all_to_all | solution.py:48
  291.5 1.7 reduce_sum.81
  293.2 0.8 fusion.8
  (26 shorter events, 1.8 us)
Async XLA Ops:
  0.6 29.9 %copy-start = (bf16[2048,512]{1,0:T(8,128)(2,1)S(1)}, bf16[2048,512]{1,0:T(8,128)(2,1)}, u32[]{:S(2)}) copy-start(bf16[2048,512]{1,0:T(8,128)(2,1)} %param.8) | copy-start | bytes 6291460
  29.1 1.4 copy-start.5
  29.1 1.4 copy-start.6
  30.6 23.1 %copy-start.1 = (bf16[512,256]{1,0:T(8,128)(2,1)S(1)}, bf16[512,256]{1,0:T(8,128)(2,1)}, u32[]{:S(2)}) copy-start(bf16[512,256]{1,0:T(8,128)(2,1)} %param.10) | copy-start | bytes 786436
  33.9 31.1 %copy-start.4 = (f32[32,256]{1,0:T(8,128)S(1)}, f32[32,256]{1,0:T(8,128)}, u32[]{:S(2)}) copy-start(f32[32,256]{1,0:T(8,128)} %param.11) | copy-start | bytes 98308
  65.0 16.8 %copy-start.3 = (f32[32,256]{1,0:T(8,128)}, f32[32,256]{1,0:T(8,128)S(1)}, u32[]{:S(2)}) copy-start(f32[32,256]{1,0:T(8,128)S(1)} %reduce_sum.76) | copy-start | bytes 98308
  291.5 1.7 copy-start.2
where the time goes:
time: 295 us; the launch traced here: 294 us
  blocking collectives  247 us (84%)
  matrix products  21.9 us (7%)
  local copies, waits for them, and re-layouts  16.3 us (6%)
  other arithmetic  7.76 us (3%)
    all_to_all x6, blocking collectives, sent_to_all(): lax.all_to_all(jnp.broadcast_to(value[None], (length, *value.shape)), axi...  132 us
    all_to_all x4, blocking collectives, sent_and_summed(): lax.all_to_all(blocks, axis, split_axis=0, concat_axis=0, tiled=True)  103 us
    dot_general x4, matrix products, on_device(): jnp.einsum('wnp,mp->wnm', mixed, interp, preferred_element_type=jnp.float32)  18 us
    unnamed x22, local copies, waits for them, and re-layouts  13.3 us
    all_to_all x1, blocking collectives, sum_at_owner(): lax.all_to_all(cut_along(value, dim, length), axis, 0, 0, tiled=True)  11.8 us
    reduce_sum x4, other arithmetic, sent_and_summed(): return arrived.astype(jnp.float32).sum(axis=0)  6.85 us

commit v1 on v0

v1 whole, which is shorter than its diff:
```python
import jax
import jax.numpy as jnp
from jax import lax
from jax.experimental import pallas as pl
from jax.experimental.pallas import tpu as pltpu
from jax.sharding import PartitionSpec as P

TERMS = 4
TIME_ROOT = 2.2
MESH = pl.DeviceIdType.MESH
F32, BF16 = jnp.float32, jnp.bfloat16

NX, NZ, NY = 4, 8, 4
WALK, CHOL = NX * NZ, NY * 2
ROWS, BASIS, PTS, VEC = 400, 2048, 512, 256
COLS = BASIS // CHOL
WIN, STEP = 112, 96
XROWS, ZROWS = 256, 128
ZBASE = NX * XROWS
TILE = 512
TILES = BASIS // TILE


def three_parts(value):
    high = value.astype(BF16)
    rest = value - high.astype(F32)
    middle = rest.astype(BF16)
    low = (rest - middle.astype(F32)).astype(BF16)
    return jnp.concatenate([high, middle, low], axis=0)


def sum_of_parts(value, rows):
    return value[:rows] + value[rows : 2 * rows] + value[2 * rows :]


def dot(left, right):
    return jnp.dot(left, right, preferred_element_type=F32)


def dot_last(left, right):
    return lax.dot_general(left, right, (((1,), (1,)), ((), ())), preferred_element_type=F32)


def kernel(
    orb_in, inv_in, interp_in, occ_in, chol_in, fields_in,
    out, bias_out,
    ip, orb, inv, occ, chol, fields,
    gathered, product, weights, bias_parts, bias, field_part, scale_in, scales,
    current, mixed, own_part, other_part, term, total, send_out, recv_out,
    load_sem, gather_send, gather_recv, orb_send, orb_recv,
    small_send, small_recv, part_send, part_recv, out_send, out_recv, store_sem,
):
    walk, place = lax.axis_index("walk"), lax.axis_index("chol")
    x, z = lax.rem(walk, NX), lax.div(walk, NX)
    core, y = lax.rem(place, 2), lax.div(place, 2)

    def at_y(step):
        return lax.rem(y + step + NY, NY)

    def chol_of(step):
        return at_y(step) * 2 + core

    def on_x(step):
        return {"walk": z * NX + lax.rem(x + step + NX, NX), "chol": place}

    def on_z(step):
        return {"walk": lax.rem(z + step + NZ, NZ) * NX + x, "chol": place}

    def on_y(step):
        return {"walk": walk, "chol": chol_of(step)}

    partner = {"walk": walk, "chol": y * 2 + (1 - core)}

    barrier = pltpu.get_barrier_semaphore()

    def greet_walk(step, carry):
        pl.semaphore_signal(
            barrier, inc=1,
            device_id={"walk": lax.rem(walk + step, WALK), "chol": place}, device_id_type=MESH,
        )
        return carry

    def greet_chol(step, carry):
        pl.semaphore_signal(
            barrier, inc=1,
            device_id={"walk": walk, "chol": lax.rem(place + step, CHOL)}, device_id_type=MESH,
        )
        return carry

    lax.fori_loop(1, WALK, greet_walk, 0)
    lax.fori_loop(1, CHOL, greet_chol, 0)
    loads = [
        pltpu.make_async_copy(orb_in.at[0], orb.at[place], load_sem.at[0]),
        pltpu.make_async_copy(interp_in, ip.at[y], load_sem.at[1]),
        pltpu.make_async_copy(inv_in.at[0], inv, load_sem.at[2]),
        pltpu.make_async_copy(occ_in, occ, load_sem.at[3]),
        pltpu.make_async_copy(chol_in, chol, load_sem.at[4]),
        pltpu.make_async_copy(fields_in, fields, load_sem.at[5]),
    ]
    for load in loads:
        load.start()
    loads[2].wait()
    loads[3].wait()
    gathered[...] = lax.dot_general(
        inv[...], occ[...], (((0,), (0,)), ((), ())), preferred_element_type=F32
    )
    loads[0].wait()
    loads[1].wait()
    loads[4].wait()
    loads[5].wait()
    pl.semaphore_wait(barrier, WALK - 1 + CHOL - 1)

    def moved(index, block, start, count, device):
        place_of = ip.at[block, pl.ds(pl.multiple_of(start, 16), count)]
        return pltpu.make_async_remote_copy(
            src_ref=place_of, dst_ref=place_of,
            send_sem=gather_send.at[index], recv_sem=gather_recv.at[index],
            device_id=device, device_id_type=MESH,
        )

    transfers = {}

    def start_gather(name, *what):
        copy = moved(len(transfers), *what)
        transfers[name] = copy
        copy.start()

    def landed(*names):
        for name in names:
            transfers[name].wait_recv()

    x_start = x * XROWS
    z_start = ZBASE + z * ZROWS

    def x_piece(step):
        return lax.rem(x + step + NX, NX) * XROWS

    def z_piece(step):
        return ZBASE + lax.rem(z + step + NZ, NZ) * ZROWS

    def y0(kind):
        start, count = (x_start, XROWS) if kind == "x" else (z_start, ZROWS)
        for way in (1, -1):
            start_gather(("y0", kind, way), y, start, count, on_y(way))

    def y1(kind):
        start, count = (x_start, XROWS) if kind == "x" else (z_start, ZROWS)
        half = count // 2
        start_gather(("y1", kind, 1), at_y(-1), start, half, on_y(1))
        start_gather(("y1", kind, -1), at_y(1), start + half, half, on_y(-1))

    def x0(block):
        for way in (1, -1):
            start_gather(("x0", block, way), at_y(block), x_start, XROWS, on_x(way))

    def x1(block):
        half = XROWS // 2
        start_gather(("x1", block, 1), at_y(block), x_piece(-1), half, on_x(1))
        start_gather(("x1", block, -1), at_y(block), x_piece(1) + half, half, on_x(-1))

    def zs(step, block):
        for way in (1, -1):
            start_gather(
                (f"z{step}", block, way), at_y(block), z_piece(-way * step), ZROWS, on_z(way)
            )

    def z3(block):
        half = ZROWS // 2
        start_gather(("z3", block, 1), at_y(block), z_piece(-3), half, on_z(1))
        start_gather(("z3", block, -1), at_y(block), z_piece(3) + half, half, on_z(-1))

    def both(stage, block):
        landed((stage, block, 1), (stage, block, -1))

    def orb_copy(index, block, rows, device):
        place_of = orb.at[block, rows]
        return pltpu.make_async_remote_copy(
            src_ref=place_of, dst_ref=place_of,
            send_sem=orb_send.at[index], recv_sem=orb_recv.at[index],
            device_id=device, device_id_type=MESH,
        )

    everything, lower, upper = pl.ds(0, ROWS), pl.ds(0, 208), pl.ds(208, 192)
    o_up = orb_copy(0, place, everything, on_y(1))
    o_down = orb_copy(1, place, everything, on_y(-1))
    o_across = orb_copy(2, place, everything, partner)
    o_up.start()
    o_down.start()
    o_across.start()
    y0("z")

    def other(block):
        return lax.div(block, 2) * 2 + (1 - lax.rem(block, 2))

    def add_product(block, first=False):
        part = dot(orb[block], ip[y, pl.ds(pl.multiple_of(block * COLS, COLS), COLS), :])
        product[...] = part if first else product[...] + part

    below, above, far = chol_of(-1), chol_of(1), chol_of(2)
    add_product(place, True)
    o_up.wait_recv()
    o_up2 = orb_copy(3, below, lower, on_y(1))
    o_up2.start()
    o_across_below = orb_copy(4, below, everything, partner)
    o_across_below.start()
    o_down.wait_recv()
    o_down2 = orb_copy(5, above, upper, on_y(-1))
    o_down2.start()
    o_across_above = orb_copy(6, above, everything, partner)
    o_across_above.start()
    y0("x")
    o_across.wait_recv()
    add_product(other(place))
    add_product(below)
    add_product(above)
    landed(("y0", "z", 1), ("y0", "z", -1))
    zs(0, -1)
    zs(0, 1)
    y1("z")
    o_across_below.wait_recv()
    add_product(other(below))
    o_across_above.wait_recv()
    add_product(other(above))
    o_up2.wait_recv()
    o_down2.wait_recv()
    o_across_far = orb_copy(7, far, everything, partner)
    o_across_far.start()
    add_product(far)
    o_across_far.wait_recv()
    add_product(other(far))

    weights[walk] = jnp.sum(gathered[...] * product[...], axis=0, keepdims=True)

    def send_weights(step, carry):
        pltpu.make_async_remote_copy(
            src_ref=weights.at[walk], dst_ref=weights.at[walk],
            send_sem=small_send.at[0], recv_sem=small_recv.at[0],
            device_id={"walk": lax.rem(walk + step, WALK), "chol": place}, device_id_type=MESH,
        ).start()
        return carry

    lax.fori_loop(1, WALK, send_weights, 0)
    landed(("y0", "x", 1), ("y0", "x", -1))
    x0(-1)
    x0(1)
    y1("x")
    both("z0", -1)
    zs(1, -1)
    both("z0", 1)
    zs(1, 1)
    landed(("y1", "z", 1), ("y1", "z", -1))
    zs(0, 2)
    some = weights.at[pl.ds(0, WALK - 1)]
    pltpu.make_async_copy(some, some, small_recv.at[0]).wait()

    all_weights = weights[...].reshape(WALK, PTS)
    partial = sum_of_parts(dot(three_parts(all_weights), chol[...]), WALK)
    bias_parts[place] = partial

    def send_bias(step, carry):
        pltpu.make_async_remote_copy(
            src_ref=bias_parts.at[place], dst_ref=bias_parts.at[place],
            send_sem=small_send.at[1], recv_sem=small_recv.at[1],
            device_id={"walk": walk, "chol": lax.rem(place + step, CHOL)}, device_id_type=MESH,
        ).start()
        return carry

    lax.fori_loop(1, CHOL, send_bias, 0)
    both("z1", -1)
    zs(2, -1)
    both("z1", 1)
    zs(2, 1)
    both("x0", -1)
    x1(-1)
    landed(("y1", "x", 1), ("y1", "x", -1))
    x0(2)
    both("x0", 1)
    x1(1)
    some_bias = bias_parts.at[pl.ds(0, CHOL - 1)]
    pltpu.make_async_copy(some_bias, some_bias, small_recv.at[1]).wait()
    bias[...] = jnp.sum(bias_parts[...], axis=0)
    store_bias = pltpu.make_async_copy(bias, bias_out, store_sem.at[0])
    store_bias.start()

    coeff = TIME_ROOT * (fields[...] - bias[...])
    part = sum_of_parts(dot_last(three_parts(coeff), chol[...]), WALK)
    field_part[...] = part.reshape(WALK, 1, PTS)

    def send_scales(step, carry):
        to = lax.rem(walk + step, WALK)
        pltpu.make_async_remote_copy(
            src_ref=field_part.at[to], dst_ref=scale_in.at[walk],
            send_sem=small_send.at[2], recv_sem=small_recv.at[2],
            device_id={"walk": to, "chol": place}, device_id_type=MESH,
        ).start()
        return carry

    lax.fori_loop(1, WALK, send_scales, 0)
    scale_in[walk] = field_part[walk]
    both("z0", 2)
    zs(1, 2)
    both("z2", -1)
    z3(-1)
    both("z2", 1)
    z3(1)
    both("x0", 2)
    x1(2)
    some_scales = scale_in.at[pl.ds(0, WALK - 1)]
    pltpu.make_async_copy(some_scales, some_scales, small_recv.at[2]).wait()
    scales[y] = jnp.sum(scale_in[...], axis=0)
    to_up = [
        pltpu.make_async_remote_copy(
            src_ref=scales.at[y], dst_ref=scales.at[y],
            send_sem=small_send.at[3], recv_sem=small_recv.at[3],
            device_id=on_y(step), device_id_type=MESH,
        )
        for step in range(1, NY)
    ]
    for copy in to_up:
        copy.start()

    both("z1", 2)
    zs(2, 2)
    both("z2", 2)
    z3(2)
    both("x1", -1)
    both("x1", 1)
    both("x1", 2)
    both("z3", -1)
    both("z3", 1)
    both("z3", 2)

    window = pl.ds(pl.multiple_of(y * STEP, 16), WIN)
    for block in range(CHOL):
        rows = orb[block, window, :]
        term[:, block * COLS : (block + 1) * COLS] = rows
        total[:, block * COLS : (block + 1) * COLS] = rows.astype(F32)

    def multiply(block, carry):
        current[block] = dot(term[...], ip[block])
        return carry

    lax.fori_loop(0, NY, multiply, 0)
    some_blocks = scales.at[pl.ds(0, NY - 1)]
    pltpu.make_async_copy(some_blocks, some_blocks, small_recv.at[3]).wait()

    for order in range(1, TERMS + 1):
        if order > 1:
            lax.fori_loop(0, NY, multiply, 0)
        for block in range(NY):
            mixed[:, block * PTS : (block + 1) * PTS] = (
                current[block] * scales[block] / order
            ).astype(BF16)
        slot = order - 1

        def exchange(tile):
            return pltpu.make_async_remote_copy(
                src_ref=own_part.at[slot, tile], dst_ref=other_part.at[slot, tile],
                send_sem=part_send.at[slot, tile], recv_sem=part_recv.at[slot, tile],
                device_id=partner, device_id_type=MESH,
            )

        def back(tile, carry):
            rows = pl.ds(pl.multiple_of(tile * TILE, TILE), TILE)
            value = dot_last(mixed[:, 0:PTS], ip[0, rows, :])
            for block in range(1, NY):
                value += dot_last(mixed[:, block * PTS : (block + 1) * PTS], ip[block, rows, :])
            own_part[slot, tile] = value.astype(BF16)
            exchange(tile).start()
            return carry

        lax.fori_loop(0, TILES, back, 0)
        for tile in range(TILES):
            exchange(tile).wait_recv()
            columns = slice(tile * TILE, (tile + 1) * TILE)
            value = (own_part[slot, tile].astype(F32) + other_part[slot, tile].astype(F32)).astype(BF16)
            term[:, columns] = value
            total[:, columns] = total[:, columns] + value.astype(F32)

    for step in (2, 1, 3, 0):
        to = at_y(step)
        columns = pl.ds(pl.multiple_of((to * 2 + core) * COLS, COLS), COLS)
        send_out[to] = total[:, columns].astype(BF16)
        if step:
            pltpu.make_async_remote_copy(
                src_ref=send_out.at[to], dst_ref=recv_out.at[y],
                send_sem=out_send, recv_sem=out_recv,
                device_id=on_y(step), device_id_type=MESH,
            ).start()
    recv_out[y] = send_out[y]
    some_out = recv_out.at[pl.ds(0, NY - 1)]
    pltpu.make_async_copy(some_out, some_out, out_recv).wait()
    stores = []
    for part in range(NY):
        count = WIN if part == NY - 1 else STEP
        stores.append(
            pltpu.make_async_copy(
                recv_out.at[part, pl.ds(0, count)], out.at[0, pl.ds(part * STEP, count)],
                store_sem.at[1 + part],
            )
        )
    for store in stores:
        store.start()

    for copy in transfers.values():
        copy.wait_send()
    for copy in (o_up, o_down, o_across, o_up2, o_down2, o_across_below, o_across_above, o_across_far):
        copy.wait_send()
    pltpu.make_async_copy(some, some, small_send.at[0]).wait()
    pltpu.make_async_copy(some_bias, some_bias, small_send.at[1]).wait()
    pltpu.make_async_copy(some_scales, some_scales, small_send.at[2]).wait()
    pltpu.make_async_copy(some_blocks, some_blocks, small_send.at[3]).wait()
    for slot in range(TERMS):
        for tile in range(TILES):
            pltpu.make_async_copy(
                own_part.at[slot, tile], other_part.at[slot, tile], part_send.at[slot, tile]
            ).wait()
    pltpu.make_async_copy(some_out, some_out, out_send).wait()
    store_bias.wait()
    for store in stores:
        store.wait()


N_GATHER = 8 + 12 + 24


def on_device(orbitals, intersection_inv, interp, occ_interp, chol_factors, fields):
    dma = pltpu.SemaphoreType.DMA
    hbm = pl.BlockSpec(memory_space=pl.ANY)
    return pl.pallas_call(
        kernel,
        out_shape=(
            jax.ShapeDtypeStruct((1, ROWS, COLS), BF16),
            jax.ShapeDtypeStruct((WALK, VEC), F32),
        ),
        in_specs=[hbm] * 6,
        out_specs=(hbm, hbm),
        scratch_shapes=[
            pltpu.VMEM((NY, BASIS, PTS), BF16),
            pltpu.VMEM((CHOL, ROWS, COLS), BF16),
            pltpu.VMEM((ROWS, ROWS), BF16),
            pltpu.VMEM((ROWS, PTS), BF16),
            pltpu.VMEM((PTS, VEC), BF16),
            pltpu.VMEM((WALK, VEC), F32),
            pltpu.VMEM((ROWS, PTS), F32),
            pltpu.VMEM((ROWS, PTS), F32),
            pltpu.VMEM((WALK, 1, PTS), F32),
            pltpu.VMEM((CHOL, WALK, VEC), F32),
            pltpu.VMEM((WALK, VEC), F32),
            pltpu.VMEM((WALK, 1, PTS), F32),
            pltpu.VMEM((WALK, 1, PTS), F32),
            pltpu.VMEM((NY, 1, PTS), F32),
            pltpu.VMEM((NY, WIN, PTS), F32),
            pltpu.VMEM((WIN, NY * PTS), BF16),
            pltpu.VMEM((TERMS, TILES, WIN, TILE), BF16),
            pltpu.VMEM((TERMS, TILES, WIN, TILE), BF16),
            pltpu.VMEM((WIN, BASIS), BF16),
            pltpu.VMEM((WIN, BASIS), F32),
            pltpu.VMEM((NY, WIN, COLS), BF16),
            pltpu.VMEM((NY, WIN, COLS), BF16),
            dma((6,)),
            dma((N_GATHER,)),
            dma((N_GATHER,)),
            dma((8,)),
            dma((8,)),
            dma((4,)),
            dma((4,)),
            dma((TERMS, TILES)),
            dma((TERMS, TILES)),
            dma,
            dma,
            dma((5,)),
        ],
        compiler_params=pltpu.CompilerParams(
            collective_id=0, has_side_effects=True, vmem_limit_bytes=60 * 1024 * 1024
        ),
    )(orbitals, intersection_inv, interp, occ_interp, chol_factors, fields)


def solution(mesh):
    placed = (
        P("walk", None, "chol"),
        P("walk", None, None),
        P(None, "chol"),
        P(None, "chol"),
        P("chol", "walk"),
        P(None, "walk"),
    )
    return jax.shard_map(
        on_device,
        mesh=mesh,
        in_specs=placed,
        out_specs=(P("walk", None, "chol"), P(None, "walk")),
        check_vma=False,
    )
```

time: 295 us -> 96.5 us (0.33)
  blocking collectives: 247 us -> 0 us
  Pallas kernels: 0 us -> 92.7 us
  matrix products: 21.9 us -> 0 us
  local copies, waits for them, and re-layouts: 16.3 us -> 3 us
  other arithmetic: 7.76 us -> 0 us
    all_to_all x11 -> x0, blocking collectives: 247 us -> none  [the longest x6 132 us: sent_to_all(): lax.all_to_all(jnp.broadcast_to(value[None], (length, *value.shape)), axi...]
    pallas_call x0 -> x1, Pallas kernels: none -> 92.7 us  [on_device(): pl.pallas_call(kernel, out_shape=(jax.ShapeDtypeStruct((1, ROWS, COLS), B...]
    dot_general x7 -> x0, matrix products: 21.9 us -> none  [the longest x4 18 us: on_device(): jnp.einsum('wnp,mp->wnm', mixed, interp, preferred_element_type=jnp.float32)]
    unnamed x22 -> x2, local copies, waits for them, and re-layouts: 13.3 us -> 3 us
    reduce_sum x6 -> x0, other arithmetic: 6.94 us -> none  [the longest x4 6.85 us: sent_and_summed(): return arrived.astype(jnp.float32).sum(axis=0)]
where the time goes in v1:
time: 96.5 us; the launch traced here: 96.3 us
  Pallas kernels  92.7 us (96%)
  local copies, waits for them, and re-layouts  3 us (3%)
    pallas_call x1, Pallas kernels, on_device(): pl.pallas_call(kernel, out_shape=(jax.ShapeDtypeStruct((1, ROWS, COLS), B...  92.7 us
    unnamed x2, local copies, waits for them, and re-layouts  3 us

profile of v1, /device:TPU:1, one launch (start us, length us, event | category | flops | bytes accessed | tf_op | source)
XLA Modules:
  0.0 96.3 jit_solution(9474879749276335931)
XLA Ops:
  0.6 92.7 %shard_map.77 = (bf16[1,400,256]{2,1,0:T(8,128)(2,1)}, f32[32,256]{1,0:T(8,128)}) custom-call(bf16[1,400,256]{2,1,0:T(8,128)(2,1)} %orb_in.1, bf16[1,400,400]{2,1,0:T(8,128)(2,1)} %inv_in.1, bf16[2048,512]{1,0:T(8,128)(2,1)} %interp_in.1, bf16[400,512]{1,0:T(8,128)(2,1)} %occ_in.1, bf16[512,256]{1,0:T(8,128)(2,1)} %chol_in.1, f32[32,256]{1,0:T(8,128)} %fields_in.1), custom_call_target="tpu_custom_call" | custom-call | tf_op jit(solution)/shard_map/pallas_call | solution.py:430
  93.3 1.6 %copy.10 = bf16[1,400,256]{2,1,0:T(8,128)(2,1)} copy(bf16[1,400,256]{2,1,0:T(8,128)(2,1)} %get-tuple-element.4) | data formatting | bytes 409600
  95.0 1.4 %copy.11 = f32[32,256]{1,0:T(8,128)} copy(f32[32,256]{1,0:T(8,128)} %get-tuple-element.5) | data formatting | bytes 65536

commit v2 on v1

--- a/solution.py
+++ b/solution.py
@@ -15,10 +15,14 @@
 ROWS, BASIS, PTS, VEC = 400, 2048, 512, 256
 COLS = BASIS // CHOL
 WIN, STEP = 112, 96
-XROWS, ZROWS = 256, 128
+XROWS, XHALF = 224, 112
+ZROWS, ZHALF = 96, 48
 ZBASE = NX * XROWS
+CBASE = ZBASE + NZ * ZROWS
+CROWS, CHALF = BASIS - CBASE, 192
 TILE = 512
 TILES = BASIS // TILE
+TURN = 512
 
 
 def three_parts(value):
@@ -44,8 +48,8 @@
 def kernel(
     orb_in, inv_in, interp_in, occ_in, chol_in, fields_in,
     out, bias_out,
-    ip, orb, inv, occ, chol, fields,
-    gathered, product, weights, bias_parts, bias, field_part, scale_in, scales,
+    ip, turned, orb, inv, occ, chol, fields,
+    gathered, product, weights, pair, bias_parts, bias, field_part, scale_in, scales,
     current, mixed, own_part, other_part, term, total, send_out, recv_out,
     load_sem, gather_send, gather_recv, orb_send, orb_recv,
     small_send, small_recv, part_send, part_recv, out_send, out_recv, store_sem,
@@ -106,6 +110,14 @@
     )
     loads[0].wait()
     loads[1].wait()
+
+    def turn(block, first, count):
+        points = pl.ds(pl.multiple_of(block * PTS, PTS), PTS)
+        for start in range(first, first + count, TURN):
+            rows = slice(start, min(start + TURN, first + count))
+            turned[points, rows] = ip[block, rows, :].T
+
+    turn(y, 0, BASIS)
     loads[4].wait()
     loads[5].wait()
     pl.semaphore_wait(barrier, WALK - 1 + CHOL - 1)
@@ -129,34 +141,55 @@
         for name in names:
             transfers[name].wait_recv()
 
-    x_start = x * XROWS
-    z_start = ZBASE + z * ZROWS
-
     def x_piece(step):
         return lax.rem(x + step + NX, NX) * XROWS
 
     def z_piece(step):
         return ZBASE + lax.rem(z + step + NZ, NZ) * ZROWS
 
-    def y0(kind):
-        start, count = (x_start, XROWS) if kind == "x" else (z_start, ZROWS)
-        for way in (1, -1):
-            start_gather(("y0", kind, way), y, start, count, on_y(way))
-
-    def y1(kind):
-        start, count = (x_start, XROWS) if kind == "x" else (z_start, ZROWS)
-        half = count // 2
-        start_gather(("y1", kind, 1), at_y(-1), start, half, on_y(1))
-        start_gather(("y1", kind, -1), at_y(1), start + half, half, on_y(-1))
-
-    def x0(block):
-        for way in (1, -1):
-            start_gather(("x0", block, way), at_y(block), x_start, XROWS, on_x(way))
+    def half_of(start, rows, half, way):
+        return (start, half) if way == 1 else (start + half, rows - half)
+
+    def x_half(step, way):
+        return half_of(x_piece(step), XROWS, XHALF, way)
+
+    def z_half(step, way):
+        return half_of(z_piece(step), ZROWS, ZHALF, way)
+
+    def c_half(way):
+        return half_of(CBASE, CROWS, CHALF, way)
+
+    def y0z():
+        for way in (1, -1):
+            start_gather(("y0z", way), y, z_piece(0), ZROWS, on_y(way))
+
+    def y0x(first):
+        for way in (1, -1):
+            start_gather(("y0x", first, way), y, *x_half(0, way * first), on_y(way))
+
+    def y0c(first):
+        for way in (1, -1):
+            start_gather(("y0c", first, way), y, *c_half(way * first), on_y(way))
+
+    def y1z():
+        for way in (1, -1):
+            start_gather(("y1z", way), at_y(-way), *z_half(0, way), on_y(way))
+
+    def y1x():
+        for way in (1, -1):
+            start_gather(("y1x", way), at_y(-way), *x_half(0, way), on_y(way))
+
+    def y1c():
+        for way in (1, -1):
+            start_gather(("y1c", way), at_y(-way), *c_half(way), on_y(way))
+
+    def x0(block, half):
+        for way in (half, -half):
+            start_gather(("x0", block, half, way), at_y(block), *x_half(0, half), on_x(way))
 
     def x1(block):
-        half = XROWS // 2
-        start_gather(("x1", block, 1), at_y(block), x_piece(-1), half, on_x(1))
-        start_gather(("x1", block, -1), at_y(block), x_piece(1) + half, half, on_x(-1))
+        for way in (1, -1):
+            start_gather(("x1", block, way), at_y(block), *x_half(-way, way), on_x(way))
 
     def zs(step, block):
         for way in (1, -1):
@@ -165,12 +198,11 @@
             )
 
     def z3(block):
-        half = ZROWS // 2
-        start_gather(("z3", block, 1), at_y(block), z_piece(-3), half, on_z(1))
-        start_gather(("z3", block, -1), at_y(block), z_piece(3) + half, half, on_z(-1))
-
-    def both(stage, block):
-        landed((stage, block, 1), (stage, block, -1))
+        for way in (1, -1):
+            start_gather(("z3", block, way), at_y(block), *z_half(-3 * way, way), on_z(way))
+
+    def both(*stage):
+        landed((*stage, 1), (*stage, -1))
 
     def orb_copy(index, block, rows, device):
         place_of = orb.at[block, rows]
@@ -187,7 +219,7 @@
     o_up.start()
     o_down.start()
     o_across.start()
-    y0("z")
+    y0z()
 
     def other(block):
         return lax.div(block, 2) * 2 + (1 - lax.rem(block, 2))
@@ -208,15 +240,16 @@
     o_down2.start()
     o_across_above = orb_copy(6, above, everything, partner)
     o_across_above.start()
-    y0("x")
+    y0x(1)
     o_across.wait_recv()
     add_product(other(place))
     add_product(below)
     add_product(above)
-    landed(("y0", "z", 1), ("y0", "z", -1))
+    both("y0z")
     zs(0, -1)
     zs(0, 1)
-    y1("z")
+    y1z()
+    y0x(-1)
     o_across_below.wait_recv()
     add_product(other(below))
     o_across_above.wait_recv()
@@ -240,45 +273,63 @@
         return carry
 
     lax.fori_loop(1, WALK, send_weights, 0)
-    landed(("y0", "x", 1), ("y0", "x", -1))
-    x0(-1)
-    x0(1)
-    y1("x")
+    both("y0x", 1)
+    x0(-1, 1)
+    x0(1, -1)
+    both("y1z")
+    zs(0, 2)
     both("z0", -1)
     zs(1, -1)
+    both("y0x", -1)
+    x0(-1, -1)
+    x0(1, 1)
+    y1x()
+    y0c(1)
     both("z0", 1)
     zs(1, 1)
-    landed(("y1", "z", 1), ("y1", "z", -1))
-    zs(0, 2)
+    window = pl.ds(pl.multiple_of(y * STEP, 16), WIN)
+    for block in range(CHOL):
+        rows = orb[block, window, :]
+        term[:, block * COLS : (block + 1) * COLS] = rows
+        total[:, block * COLS : (block + 1) * COLS] = rows.astype(F32)
+
+    def multiply(block):
+        current[block] = dot(term[...], ip[block])
+
+    multiply(y)
     some = weights.at[pl.ds(0, WALK - 1)]
     pltpu.make_async_copy(some, some, small_recv.at[0]).wait()
 
     all_weights = weights[...].reshape(WALK, PTS)
     partial = sum_of_parts(dot(three_parts(all_weights), chol[...]), WALK)
-    bias_parts[place] = partial
-
-    def send_bias(step, carry):
+    pair[core] = partial
+    across = pltpu.make_async_remote_copy(
+        src_ref=pair.at[core], dst_ref=pair.at[core],
+        send_sem=small_send.at[4], recv_sem=small_recv.at[4],
+        device_id=partner, device_id_type=MESH,
+    )
+    across.start()
+    both("z0", 2)
+    zs(1, 2)
+    across.wait_recv()
+    bias_parts[y] = pair[0] + pair[1]
+    for step in (2, 1, 3):
         pltpu.make_async_remote_copy(
-            src_ref=bias_parts.at[place], dst_ref=bias_parts.at[place],
+            src_ref=bias_parts.at[y], dst_ref=bias_parts.at[y],
             send_sem=small_send.at[1], recv_sem=small_recv.at[1],
-            device_id={"walk": walk, "chol": lax.rem(place + step, CHOL)}, device_id_type=MESH,
+            device_id=on_y(step), device_id_type=MESH,
         ).start()
-        return carry
-
-    lax.fori_loop(1, CHOL, send_bias, 0)
+    both("y1x")
+    x0(2, 1)
+    x0(2, -1)
     both("z1", -1)
     zs(2, -1)
     both("z1", 1)
     zs(2, 1)
-    both("x0", -1)
-    x1(-1)
-    landed(("y1", "x", 1), ("y1", "x", -1))
-    x0(2)
-    both("x0", 1)
-    x1(1)
-    some_bias = bias_parts.at[pl.ds(0, CHOL - 1)]
+    y0c(-1)
+    some_bias = bias_parts.at[pl.ds(0, NY - 1)]
     pltpu.make_async_copy(some_bias, some_bias, small_recv.at[1]).wait()
-    bias[...] = jnp.sum(bias_parts[...], axis=0)
+    bias[...] = (bias_parts[0] + bias_parts[1]) + (bias_parts[2] + bias_parts[3])
     store_bias = pltpu.make_async_copy(bias, bias_out, store_sem.at[0])
     store_bias.start()
 
@@ -297,14 +348,19 @@
 
     lax.fori_loop(1, WALK, send_scales, 0)
     scale_in[walk] = field_part[walk]
-    both("z0", 2)
-    zs(1, 2)
+    both("z1", 2)
+    zs(2, 2)
+    for half in (1, -1):
+        both("x0", -1, half)
+        both("x0", 1, half)
+    x1(-1)
+    x1(1)
+    both("y0c", 1)
+    y1c()
     both("z2", -1)
     z3(-1)
     both("z2", 1)
     z3(1)
-    both("x0", 2)
-    x1(2)
     some_scales = scale_in.at[pl.ds(0, WALK - 1)]
     pltpu.make_async_copy(some_scales, some_scales, small_recv.at[2]).wait()
     scales[y] = jnp.sum(scale_in[...], axis=0)
@@ -319,63 +375,67 @@
     for copy in to_up:
         copy.start()
 
-    both("z1", 2)
-    zs(2, 2)
     both("z2", 2)
     z3(2)
+    both("x0", 2, 1)
+    both("x0", 2, -1)
+    x1(2)
     both("x1", -1)
     both("x1", 1)
-    both("x1", 2)
     both("z3", -1)
     both("z3", 1)
+    both("y0c", -1)
+    for step in (-1, 1):
+        turn(at_y(step), 0, BASIS)
+        multiply(at_y(step))
+    both("x1", 2)
+    turn(at_y(2), 0, ZBASE)
+    both("y1c")
+    turn(at_y(2), CBASE, CROWS)
     both("z3", 2)
-
-    window = pl.ds(pl.multiple_of(y * STEP, 16), WIN)
-    for block in range(CHOL):
-        rows = orb[block, window, :]
-        term[:, block * COLS : (block + 1) * COLS] = rows
-        total[:, block * COLS : (block + 1) * COLS] = rows.astype(F32)
-
-    def multiply(block, carry):
-        current[block] = dot(term[...], ip[block])
-        return carry
-
-    lax.fori_loop(0, NY, multiply, 0)
+    turn(at_y(2), ZBASE, CBASE - ZBASE)
+    multiply(at_y(2))
     some_blocks = scales.at[pl.ds(0, NY - 1)]
     pltpu.make_async_copy(some_blocks, some_blocks, small_recv.at[3]).wait()
 
-    for order in range(1, TERMS + 1):
-        if order > 1:
-            lax.fori_loop(0, NY, multiply, 0)
+    def exchange(slot, tile):
+        return pltpu.make_async_remote_copy(
+            src_ref=own_part.at[slot, tile], dst_ref=other_part.at[slot, tile],
+            send_sem=part_send.at[slot, tile], recv_sem=part_recv.at[slot, tile],
+            device_id=partner, device_id_type=MESH,
+        )
+
+    def points_to_basis(slot):
         for block in range(NY):
             mixed[:, block * PTS : (block + 1) * PTS] = (
-                current[block] * scales[block] / order
+                current[block] * (scales[block] / (slot + 1).astype(F32))
             ).astype(BF16)
-        slot = order - 1
-
-        def exchange(tile):
-            return pltpu.make_async_remote_copy(
-                src_ref=own_part.at[slot, tile], dst_ref=other_part.at[slot, tile],
-                send_sem=part_send.at[slot, tile], recv_sem=part_recv.at[slot, tile],
-                device_id=partner, device_id_type=MESH,
-            )
-
-        def back(tile, carry):
-            rows = pl.ds(pl.multiple_of(tile * TILE, TILE), TILE)
-            value = dot_last(mixed[:, 0:PTS], ip[0, rows, :])
-            for block in range(1, NY):
-                value += dot_last(mixed[:, block * PTS : (block + 1) * PTS], ip[block, rows, :])
-            own_part[slot, tile] = value.astype(BF16)
-            exchange(tile).start()
-            return carry
-
-        lax.fori_loop(0, TILES, back, 0)
+
         for tile in range(TILES):
-            exchange(tile).wait_recv()
             columns = slice(tile * TILE, (tile + 1) * TILE)
-            value = (own_part[slot, tile].astype(F32) + other_part[slot, tile].astype(F32)).astype(BF16)
-            term[:, columns] = value
-            total[:, columns] = total[:, columns] + value.astype(F32)
+            own_part[slot, tile] = dot(mixed[...], turned[:, columns]).astype(BF16)
+            exchange(slot, tile).start()
+
+    def summed(slot, tile):
+        exchange(slot, tile).wait_recv()
+        columns = slice(tile * TILE, (tile + 1) * TILE)
+        value = (own_part[slot, tile].astype(F32) + other_part[slot, tile].astype(F32)).astype(BF16)
+        total[:, columns] = total[:, columns] + value.astype(F32)
+        return value
+
+    def one_term(slot, carry):
+        points_to_basis(slot)
+        for tile in range(TILES):
+            value = summed(slot, tile)
+            for block in range(NY):
+                part = dot(value, ip[block, tile * TILE : (tile + 1) * TILE, :])
+                current[block] = current[block] + part if tile else part
+        return carry
+
+    lax.fori_loop(0, TERMS - 1, one_term, 0)
+    points_to_basis(jnp.int32(TERMS - 1))
+    for tile in range(TILES):
+        summed(TERMS - 1, tile)
 
     for step in (2, 1, 3, 0):
         to = at_y(step)
@@ -388,6 +448,20 @@
                 device_id=on_y(step), device_id_type=MESH,
             ).start()
     recv_out[y] = send_out[y]
+    for copy in transfers.values():
+        copy.wait_send()
+    for copy in (o_up, o_down, o_across, o_up2, o_down2, o_across_below, o_across_above, o_across_far):
+        copy.wait_send()
+    pltpu.make_async_copy(some, some, small_send.at[0]).wait()
+    pltpu.make_async_copy(some_bias, some_bias, small_send.at[1]).wait()
+    pltpu.make_async_copy(some_scales, some_scales, small_send.at[2]).wait()
+    pltpu.make_async_copy(some_blocks, some_blocks, small_send.at[3]).wait()
+    across.wait_send()
+    for slot in range(TERMS):
+        for tile in range(TILES):
+            pltpu.make_async_copy(
+                own_part.at[slot, tile], other_part.at[slot, tile], part_send.at[slot, tile]
+            ).wait()
     some_out = recv_out.at[pl.ds(0, NY - 1)]
     pltpu.make_async_copy(some_out, some_out, out_recv).wait()
     stores = []
@@ -402,26 +476,13 @@
     for store in stores:
         store.start()
 
-    for copy in transfers.values():
-        copy.wait_send()
-    for copy in (o_up, o_down, o_across, o_up2, o_down2, o_across_below, o_across_above, o_across_far):
-        copy.wait_send()
-    pltpu.make_async_copy(some, some, small_send.at[0]).wait()
-    pltpu.make_async_copy(some_bias, some_bias, small_send.at[1]).wait()
-    pltpu.make_async_copy(some_scales, some_scales, small_send.at[2]).wait()
-    pltpu.make_async_copy(some_blocks, some_blocks, small_send.at[3]).wait()
-    for slot in range(TERMS):
-        for tile in range(TILES):
-            pltpu.make_async_copy(
-                own_part.at[slot, tile], other_part.at[slot, tile], part_send.at[slot, tile]
-            ).wait()
     pltpu.make_async_copy(some_out, some_out, out_send).wait()
     store_bias.wait()
     for store in stores:
         store.wait()
 
 
-N_GATHER = 8 + 12 + 24
+N_GATHER = 16 + 18 + 24
 
 
 def on_device(orbitals, intersection_inv, interp, occ_interp, chol_factors, fields):
@@ -437,6 +498,7 @@
         out_specs=(hbm, hbm),
         scratch_shapes=[
             pltpu.VMEM((NY, BASIS, PTS), BF16),
+            pltpu.VMEM((NY * PTS, BASIS), BF16),
             pltpu.VMEM((CHOL, ROWS, COLS), BF16),
             pltpu.VMEM((ROWS, ROWS), BF16),
             pltpu.VMEM((ROWS, PTS), BF16),
@@ -445,7 +507,8 @@
             pltpu.VMEM((ROWS, PTS), F32),
             pltpu.VMEM((ROWS, PTS), F32),
             pltpu.VMEM((WALK, 1, PTS), F32),
-            pltpu.VMEM((CHOL, WALK, VEC), F32),
+            pltpu.VMEM((2, WALK, VEC), F32),
+            pltpu.VMEM((NY, WALK, VEC), F32),
             pltpu.VMEM((WALK, VEC), F32),
             pltpu.VMEM((WALK, 1, PTS), F32),
             pltpu.VMEM((WALK, 1, PTS), F32),
@@ -463,8 +526,8 @@
             dma((N_GATHER,)),
             dma((8,)),
             dma((8,)),
-            dma((4,)),
-            dma((4,)),
+            dma((5,)),
+            dma((5,)),
             dma((TERMS, TILES)),
             dma((TERMS, TILES)),
             dma,

time: 96.5 us -> 77 us (0.80)
  Pallas kernels: 92.7 us -> 73.2 us
    pallas_call x1, Pallas kernels: 92.7 us -> 73.2 us  [on_device(): pl.pallas_call(kernel, out_shape=(jax.ShapeDtypeStruct((1, ROWS, COLS), B...]
where the time goes in v2:
time: 77 us; the launch traced here: 76.8 us
  Pallas kernels  73.2 us (95%)
  local copies, waits for them, and re-layouts  3 us (4%)
    pallas_call x1, Pallas kernels, on_device(): pl.pallas_call(kernel, out_shape=(jax.ShapeDtypeStruct((1, ROWS, COLS), B...  73.2 us
    unnamed x2, local copies, waits for them, and re-layouts  3 us

profile of v2, /device:TPU:1, one launch (start us, length us, event | category | flops | bytes accessed | tf_op | source)
XLA Modules:
  0.0 76.8 jit_solution(12966093993125464157)
XLA Ops:
  0.6 73.2 %shard_map.77 = (bf16[1,400,256]{2,1,0:T(8,128)(2,1)}, f32[32,256]{1,0:T(8,128)}) custom-call(bf16[1,400,256]{2,1,0:T(8,128)(2,1)} %orb_in.1, bf16[1,400,400]{2,1,0:T(8,128)(2,1)} %inv_in.1, bf16[2048,512]{1,0:T(8,128)(2,1)} %interp_in.1, bf16[400,512]{1,0:T(8,128)(2,1)} %occ_in.1, bf16[512,256]{1,0:T(8,128)(2,1)} %chol_in.1, f32[32,256]{1,0:T(8,128)} %fields_in.1), custom_call_target="tpu_custom_call" | custom-call | tf_op jit(solution)/shard_map/pallas_call | solution.py:491
  73.8 1.6 %copy.10 = bf16[1,400,256]{2,1,0:T(8,128)(2,1)} copy(bf16[1,400,256]{2,1,0:T(8,128)(2,1)} %get-tuple-element.4) | data formatting | bytes 409600
  75.5 1.4 %copy.11 = f32[32,256]{1,0:T(8,128)} copy(f32[32,256]{1,0:T(8,128)} %get-tuple-element.5) | data formatting | bytes 65536

commit v3 on v2

--- a/solution.py
+++ b/solution.py
@@ -15,8 +15,8 @@
 ROWS, BASIS, PTS, VEC = 400, 2048, 512, 256
 COLS = BASIS // CHOL
 WIN, STEP = 112, 96
-XROWS, XHALF = 224, 112
-ZROWS, ZHALF = 96, 48
+XROWS, XHALF = 192, 96
+ZROWS, ZHALF = 112, 64
 ZBASE = NX * XROWS
 CBASE = ZBASE + NZ * ZROWS
 CROWS, CHALF = BASIS - CBASE, 192
@@ -47,12 +47,12 @@
 
 def kernel(
     orb_in, inv_in, interp_in, occ_in, chol_in, fields_in,
-    out, bias_out,
+    recv_out, bias,
     ip, turned, orb, inv, occ, chol, fields,
-    gathered, product, weights, pair, bias_parts, bias, field_part, scale_in, scales,
-    current, mixed, own_part, other_part, term, total, send_out, recv_out,
+    gathered, product, weights, pair, bias_parts, field_part, scale_in, scales,
+    current, mixed, own_part, other_part, term, total, send_out,
     load_sem, gather_send, gather_recv, orb_send, orb_recv,
-    small_send, small_recv, part_send, part_recv, out_send, out_recv, store_sem,
+    small_send, small_recv, part_send, part_recv, out_send, out_recv,
 ):
     walk, place = lax.axis_index("walk"), lax.axis_index("chol")
     x, z = lax.rem(walk, NX), lax.div(walk, NX)
@@ -103,23 +103,14 @@
     ]
     for load in loads:
         load.start()
-    loads[2].wait()
-    loads[3].wait()
-    gathered[...] = lax.dot_general(
-        inv[...], occ[...], (((0,), (0,)), ((), ())), preferred_element_type=F32
-    )
-    loads[0].wait()
-    loads[1].wait()
-
     def turn(block, first, count):
         points = pl.ds(pl.multiple_of(block * PTS, PTS), PTS)
         for start in range(first, first + count, TURN):
             rows = slice(start, min(start + TURN, first + count))
             turned[points, rows] = ip[block, rows, :].T
 
-    turn(y, 0, BASIS)
-    loads[4].wait()
-    loads[5].wait()
+    loads[0].wait()
+    loads[1].wait()
     pl.semaphore_wait(barrier, WALK - 1 + CHOL - 1)
 
     def moved(index, block, start, count, device):
@@ -213,13 +204,13 @@
         )
 
     everything, lower, upper = pl.ds(0, ROWS), pl.ds(0, 208), pl.ds(208, 192)
-    o_up = orb_copy(0, place, everything, on_y(1))
-    o_down = orb_copy(1, place, everything, on_y(-1))
-    o_across = orb_copy(2, place, everything, partner)
-    o_up.start()
-    o_down.start()
-    o_across.start()
+    below, above, far = chol_of(-1), chol_of(1), chol_of(2)
+    o_up = [orb_copy(0, place, lower, on_y(1)), orb_copy(1, place, upper, on_y(1))]
+    o_down = [orb_copy(2, place, upper, on_y(-1)), orb_copy(3, place, lower, on_y(-1))]
+    o_across = orb_copy(4, place, everything, partner)
     y0z()
+    for copy in (o_up[0], o_down[0], o_up[1], o_down[1], o_across):
+        copy.start()
 
     def other(block):
         return lax.div(block, 2) * 2 + (1 - lax.rem(block, 2))
@@ -228,37 +219,48 @@
         part = dot(orb[block], ip[y, pl.ds(pl.multiple_of(block * COLS, COLS), COLS), :])
         product[...] = part if first else product[...] + part
 
-    below, above, far = chol_of(-1), chol_of(1), chol_of(2)
+    for load in loads[2:]:
+        load.wait()
+    gathered[...] = lax.dot_general(
+        inv[...], occ[...], (((0,), (0,)), ((), ())), preferred_element_type=F32
+    )
     add_product(place, True)
-    o_up.wait_recv()
-    o_up2 = orb_copy(3, below, lower, on_y(1))
-    o_up2.start()
-    o_across_below = orb_copy(4, below, everything, partner)
-    o_across_below.start()
-    o_down.wait_recv()
-    o_down2 = orb_copy(5, above, upper, on_y(-1))
-    o_down2.start()
-    o_across_above = orb_copy(6, above, everything, partner)
-    o_across_above.start()
-    y0x(1)
-    o_across.wait_recv()
-    add_product(other(place))
-    add_product(below)
-    add_product(above)
     both("y0z")
     zs(0, -1)
     zs(0, 1)
+    o_up[0].wait_recv()
+    o_up2 = orb_copy(5, below, lower, on_y(1))
+    o_up2.start()
+    o_down[0].wait_recv()
+    o_down2 = orb_copy(6, above, upper, on_y(-1))
+    o_down2.start()
     y1z()
-    y0x(-1)
+    y0x(1)
+    turn(y, 0, BASIS)
+    o_up[1].wait_recv()
+    o_across_below = orb_copy(7, below, everything, partner)
+    o_across_below.start()
+    o_down[1].wait_recv()
+    o_across_above = orb_copy(8, above, everything, partner)
+    o_across_above.start()
+    o_across.wait_recv()
+    add_product(other(place))
+    both("z0", -1)
+    zs(1, -1)
+    add_product(below)
+    add_product(above)
     o_across_below.wait_recv()
     add_product(other(below))
     o_across_above.wait_recv()
     add_product(other(above))
     o_up2.wait_recv()
     o_down2.wait_recv()
-    o_across_far = orb_copy(7, far, everything, partner)
+    o_across_far = orb_copy(9, far, everything, partner)
     o_across_far.start()
+    both("z0", 1)
+    zs(1, 1)
     add_product(far)
+    y0x(-1)
     o_across_far.wait_recv()
     add_product(other(far))
 
@@ -273,20 +275,20 @@
         return carry
 
     lax.fori_loop(1, WALK, send_weights, 0)
+    both("y1z")
+    zs(0, 2)
     both("y0x", 1)
     x0(-1, 1)
     x0(1, -1)
-    both("y1z")
-    zs(0, 2)
-    both("z0", -1)
-    zs(1, -1)
+    both("z1", -1)
+    zs(2, -1)
+    both("z1", 1)
+    zs(2, 1)
     both("y0x", -1)
     x0(-1, -1)
     x0(1, 1)
     y1x()
     y0c(1)
-    both("z0", 1)
-    zs(1, 1)
     window = pl.ds(pl.multiple_of(y * STEP, 16), WIN)
     for block in range(CHOL):
         rows = orb[block, window, :]
@@ -322,16 +324,14 @@
     both("y1x")
     x0(2, 1)
     x0(2, -1)
-    both("z1", -1)
-    zs(2, -1)
-    both("z1", 1)
-    zs(2, 1)
+    both("z2", -1)
+    z3(-1)
+    both("z2", 1)
+    z3(1)
     y0c(-1)
     some_bias = bias_parts.at[pl.ds(0, NY - 1)]
     pltpu.make_async_copy(some_bias, some_bias, small_recv.at[1]).wait()
     bias[...] = (bias_parts[0] + bias_parts[1]) + (bias_parts[2] + bias_parts[3])
-    store_bias = pltpu.make_async_copy(bias, bias_out, store_sem.at[0])
-    store_bias.start()
 
     coeff = TIME_ROOT * (fields[...] - bias[...])
     part = sum_of_parts(dot_last(three_parts(coeff), chol[...]), WALK)
@@ -357,10 +357,18 @@
     x1(1)
     both("y0c", 1)
     y1c()
-    both("z2", -1)
-    z3(-1)
-    both("z2", 1)
-    z3(1)
+    both("x0", 2, 1)
+    both("x0", 2, -1)
+    x1(2)
+    both("z3", -1)
+    both("z3", 1)
+    for step in (-1, 1):
+        turn(at_y(step), ZBASE, CBASE - ZBASE)
+    both("z2", 2)
+    z3(2)
+    both("y0c", -1)
+    for step in (-1, 1):
+        turn(at_y(step), CBASE, CROWS)
     some_scales = scale_in.at[pl.ds(0, WALK - 1)]
     pltpu.make_async_copy(some_scales, some_scales, small_recv.at[2]).wait()
     scales[y] = jnp.sum(scale_in[...], axis=0)
@@ -375,25 +383,16 @@
     for copy in to_up:
         copy.start()
 
-    both("z2", 2)
-    z3(2)
-    both("x0", 2, 1)
-    both("x0", 2, -1)
-    x1(2)
     both("x1", -1)
     both("x1", 1)
-    both("z3", -1)
-    both("z3", 1)
-    both("y0c", -1)
     for step in (-1, 1):
-        turn(at_y(step), 0, BASIS)
+        turn(at_y(step), 0, ZBASE)
         multiply(at_y(step))
+    both("y1c")
+    both("z3", 2)
+    turn(at_y(2), ZBASE, BASIS - ZBASE)
     both("x1", 2)
     turn(at_y(2), 0, ZBASE)
-    both("y1c")
-    turn(at_y(2), CBASE, CROWS)
-    both("z3", 2)
-    turn(at_y(2), ZBASE, CBASE - ZBASE)
     multiply(at_y(2))
     some_blocks = scales.at[pl.ds(0, NY - 1)]
     pltpu.make_async_copy(some_blocks, some_blocks, small_recv.at[3]).wait()
@@ -405,12 +404,14 @@
             device_id=partner, device_id_type=MESH,
         )
 
-    def points_to_basis(slot):
+    def mix(slot):
         for block in range(NY):
             mixed[:, block * PTS : (block + 1) * PTS] = (
                 current[block] * (scales[block] / (slot + 1).astype(F32))
             ).astype(BF16)
 
+    def points_to_basis(slot):
+        mix(slot)
         for tile in range(TILES):
             columns = slice(tile * TILE, (tile + 1) * TILE)
             own_part[slot, tile] = dot(mixed[...], turned[:, columns]).astype(BF16)
@@ -433,24 +434,51 @@
         return carry
 
     lax.fori_loop(0, TERMS - 1, one_term, 0)
-    points_to_basis(jnp.int32(TERMS - 1))
-    for tile in range(TILES):
-        summed(TERMS - 1, tile)
-
-    for step in (2, 1, 3, 0):
+    last = TERMS - 1
+    mix(jnp.int32(last))
+    mine = pl.ds(pl.multiple_of(core * COLS, COLS), COLS)
+    others = pl.ds(pl.multiple_of((1 - core) * COLS, COLS), COLS)
+
+    def exchange_half(tile):
+        return pltpu.make_async_remote_copy(
+            src_ref=own_part.at[last, tile, :, others], dst_ref=other_part.at[last, tile, :, others],
+            send_sem=part_send.at[last, tile], recv_sem=part_recv.at[last, tile],
+            device_id=partner, device_id_type=MESH,
+        )
+
+    def begin(step):
         to = at_y(step)
-        columns = pl.ds(pl.multiple_of((to * 2 + core) * COLS, COLS), COLS)
-        send_out[to] = total[:, columns].astype(BF16)
+        columns = pl.ds(pl.multiple_of(to * TILE, TILE), TILE)
+        own_part[last, to] = dot(mixed[...], turned[:, columns]).astype(BF16)
+        exchange_half(to).start()
+
+    def finish(step):
+        to = at_y(step)
+        exchange_half(to).wait_recv()
+        value = own_part[last, to, :, mine].astype(F32) + other_part[last, to, :, mine].astype(F32)
+        columns = pl.ds(pl.multiple_of(to * TILE + core * COLS, COLS), COLS)
+        row = (total[:, columns] + value.astype(BF16).astype(F32)).astype(BF16)
         if step:
+            send_out[to] = row
             pltpu.make_async_remote_copy(
                 src_ref=send_out.at[to], dst_ref=recv_out.at[y],
                 send_sem=out_send, recv_sem=out_recv,
                 device_id=on_y(step), device_id_type=MESH,
             ).start()
-    recv_out[y] = send_out[y]
+        else:
+            recv_out[y] = row
+
+    begin(2)
+    begin(1)
+    begin(3)
+    finish(2)
+    finish(1)
+    begin(0)
+    finish(3)
+    finish(0)
     for copy in transfers.values():
         copy.wait_send()
-    for copy in (o_up, o_down, o_across, o_up2, o_down2, o_across_below, o_across_above, o_across_far):
+    for copy in (*o_up, *o_down, o_across, o_up2, o_down2, o_across_below, o_across_above, o_across_far):
         copy.wait_send()
     pltpu.make_async_copy(some, some, small_send.at[0]).wait()
     pltpu.make_async_copy(some_bias, some_bias, small_send.at[1]).wait()
@@ -459,27 +487,17 @@
     across.wait_send()
     for slot in range(TERMS):
         for tile in range(TILES):
-            pltpu.make_async_copy(
-                own_part.at[slot, tile], other_part.at[slot, tile], part_send.at[slot, tile]
-            ).wait()
+            (exchange if slot < last else lambda _, to: exchange_half(to))(slot, tile).wait_send()
     some_out = recv_out.at[pl.ds(0, NY - 1)]
     pltpu.make_async_copy(some_out, some_out, out_recv).wait()
-    stores = []
+    pltpu.make_async_copy(some_out, some_out, out_send).wait()
+
+
+def assemble(parts, bias_in, out, bias_out):
     for part in range(NY):
         count = WIN if part == NY - 1 else STEP
-        stores.append(
-            pltpu.make_async_copy(
-                recv_out.at[part, pl.ds(0, count)], out.at[0, pl.ds(part * STEP, count)],
-                store_sem.at[1 + part],
-            )
-        )
-    for store in stores:
-        store.start()
-
-    pltpu.make_async_copy(some_out, some_out, out_send).wait()
-    store_bias.wait()
-    for store in stores:
-        store.wait()
+        out[0, part * STEP : part * STEP + count] = parts[part, :count]
+    bias_out[...] = bias_in[...]
 
 
 N_GATHER = 16 + 18 + 24
@@ -487,15 +505,16 @@
 
 def on_device(orbitals, intersection_inv, interp, occ_interp, chol_factors, fields):
     dma = pltpu.SemaphoreType.DMA
-    hbm = pl.BlockSpec(memory_space=pl.ANY)
-    return pl.pallas_call(
+    hbm = pl.BlockSpec(memory_space=pltpu.HBM)
+    vmem = pl.BlockSpec(memory_space=pltpu.VMEM)
+    pieces = pl.pallas_call(
         kernel,
         out_shape=(
-            jax.ShapeDtypeStruct((1, ROWS, COLS), BF16),
+            jax.ShapeDtypeStruct((NY, WIN, COLS), BF16),
             jax.ShapeDtypeStruct((WALK, VEC), F32),
         ),
         in_specs=[hbm] * 6,
-        out_specs=(hbm, hbm),
+        out_specs=(vmem, vmem),
         scratch_shapes=[
             pltpu.VMEM((NY, BASIS, PTS), BF16),
             pltpu.VMEM((NY * PTS, BASIS), BF16),
@@ -509,7 +528,6 @@
             pltpu.VMEM((WALK, 1, PTS), F32),
             pltpu.VMEM((2, WALK, VEC), F32),
             pltpu.VMEM((NY, WALK, VEC), F32),
-            pltpu.VMEM((WALK, VEC), F32),
             pltpu.VMEM((WALK, 1, PTS), F32),
             pltpu.VMEM((WALK, 1, PTS), F32),
             pltpu.VMEM((NY, 1, PTS), F32),
@@ -520,24 +538,37 @@
             pltpu.VMEM((WIN, BASIS), BF16),
             pltpu.VMEM((WIN, BASIS), F32),
             pltpu.VMEM((NY, WIN, COLS), BF16),
-            pltpu.VMEM((NY, WIN, COLS), BF16),
             dma((6,)),
             dma((N_GATHER,)),
             dma((N_GATHER,)),
-            dma((8,)),
-            dma((8,)),
+            dma((10,)),
+            dma((10,)),
             dma((5,)),
             dma((5,)),
             dma((TERMS, TILES)),
             dma((TERMS, TILES)),
             dma,
             dma,
-            dma((5,)),
         ],
         compiler_params=pltpu.CompilerParams(
-            collective_id=0, has_side_effects=True, vmem_limit_bytes=60 * 1024 * 1024
+            collective_id=0, has_side_effects=True, vmem_limit_bytes=44 * 1024 * 1024
         ),
-    )(orbitals, intersection_inv, interp, occ_interp, chol_factors, fields)
+    )(
+        *(
+            pltpu.with_memory_space_constraint(value, pltpu.HBM)
+            for value in (orbitals, intersection_inv, interp, occ_interp, chol_factors, fields)
+        )
+    )
+    return pl.pallas_call(
+        assemble,
+        out_shape=(
+            jax.ShapeDtypeStruct((1, ROWS, COLS), BF16),
+            jax.ShapeDtypeStruct((WALK, VEC), F32),
+        ),
+        in_specs=[vmem] * 2,
+        out_specs=(vmem, vmem),
+        compiler_params=pltpu.CompilerParams(vmem_limit_bytes=8 * 1024 * 1024),
+    )(*pieces)
 
 
 def solution(mesh):

time: 77 us -> 71 us (0.922)
  local copies, waits for them, and re-layouts: 3 us -> 0 us
  Pallas kernels: 73.2 us -> 70.3 us
    unnamed x2 -> x0, local copies, waits for them, and re-layouts: 3 us -> none
    pallas_call x1 -> x2, Pallas kernels: 73.2 us -> 70.3 us  [the longest x1 69.6 us: on_device(): pl.pallas_call(kernel, out_shape=(jax.ShapeDtypeStruct((NY, WIN, COLS), B...]
where the time goes in v3:
time: 71 us
  Pallas kernels  70.3 us (99%)
    pallas_call x1, Pallas kernels, on_device(): pl.pallas_call(kernel, out_shape=(jax.ShapeDtypeStruct((NY, WIN, COLS), B...  69.6 us

profile of v3, /device:TPU:1, one launch (start us, length us, event | category | flops | bytes accessed | tf_op | source)
XLA Modules:
  0.0 71.0 jit_solution(15352427168467132810)
XLA Ops:
  0.6 69.6 %shard_map.77 = (bf16[4,112,256]{2,1,0:T(8,128)(2,1)S(1)}, f32[32,256]{1,0:T(8,128)S(1)}) custom-call(bf16[1,400,256]{2,1,0:T(8,128)(2,1)} %orb_in.1, bf16[1,400,400]{2,1,0:T(8,128)(2,1)} %inv_in.1, bf16[2048,512]{1,0:T(8,128)(2,1)} %interp_in.1, bf16[400,512]{1,0:T(8,128)(2,1)} %occ_in.1, bf16[512,256]{1,0:T(8,128)(2,1)} %chol_in.1, f32[32,256]{1,0:T(8,128)} %fields_in.1), custom_call_target="tpu_custom_call" | custom-call | tf_op jit(solution)/shard_map/pallas_call | solution.py:510
  70.3 0.7 shard_map.78

commit v4 on v3

--- a/solution.py
+++ b/solution.py
@@ -52,7 +52,7 @@
     gathered, product, weights, pair, bias_parts, field_part, scale_in, scales,
     current, mixed, own_part, other_part, term, total, send_out,
     load_sem, gather_send, gather_recv, orb_send, orb_recv,
-    small_send, small_recv, part_send, part_recv, out_send, out_recv,
+    small_send, small_recv, part_send, part_recv, out_send, out_recv, ready,
 ):
     walk, place = lax.axis_index("walk"), lax.axis_index("chol")
     x, z = lax.rem(walk, NX), lax.div(walk, NX)
@@ -77,22 +77,6 @@
 
     barrier = pltpu.get_barrier_semaphore()
 
-    def greet_walk(step, carry):
-        pl.semaphore_signal(
-            barrier, inc=1,
-            device_id={"walk": lax.rem(walk + step, WALK), "chol": place}, device_id_type=MESH,
-        )
-        return carry
-
-    def greet_chol(step, carry):
-        pl.semaphore_signal(
-            barrier, inc=1,
-            device_id={"walk": walk, "chol": lax.rem(place + step, CHOL)}, device_id_type=MESH,
-        )
-        return carry
-
-    lax.fori_loop(1, WALK, greet_walk, 0)
-    lax.fori_loop(1, CHOL, greet_chol, 0)
     loads = [
         pltpu.make_async_copy(orb_in.at[0], orb.at[place], load_sem.at[0]),
         pltpu.make_async_copy(interp_in, ip.at[y], load_sem.at[1]),
@@ -103,15 +87,36 @@
     ]
     for load in loads:
         load.start()
+    neighbours = [on_x(1), on_x(-1), on_z(1), on_z(-1)]
+
+    def greet(step, carry):
+        pl.semaphore_signal(
+            barrier, inc=1,
+            device_id={"walk": walk, "chol": lax.rem(place + step, CHOL)}, device_id_type=MESH,
+        )
+        return carry
+
+    for device in neighbours:
+        pl.semaphore_signal(barrier, inc=1, device_id=device, device_id_type=MESH)
+    lax.fori_loop(1, CHOL, greet, 0)
+
+    def tell(index, devices):
+        for device in devices:
+            pl.semaphore_signal(ready.at[index], inc=1, device_id=device, device_id_type=MESH)
+
+    def pass_on(index):
+        pl.semaphore_wait(ready.at[index], 2)
+        if index < NZ // 2:
+            tell(index + 1, neighbours[2:])
     def turn(block, first, count):
         points = pl.ds(pl.multiple_of(block * PTS, PTS), PTS)
         for start in range(first, first + count, TURN):
             rows = slice(start, min(start + TURN, first + count))
             turned[points, rows] = ip[block, rows, :].T
 
+    pl.semaphore_wait(barrier, CHOL - 1 + len(neighbours))
     loads[0].wait()
     loads[1].wait()
-    pl.semaphore_wait(barrier, WALK - 1 + CHOL - 1)
 
     def moved(index, block, start, count, device):
         place_of = ip.at[block, pl.ds(pl.multiple_of(start, 16), count)]
@@ -211,6 +216,7 @@
     y0z()
     for copy in (o_up[0], o_down[0], o_up[1], o_down[1], o_across):
         copy.start()
+    tell(0, neighbours[:2])
 
     def other(block):
         return lax.div(block, 2) * 2 + (1 - lax.rem(block, 2))
@@ -225,6 +231,7 @@
         inv[...], occ[...], (((0,), (0,)), ((), ())), preferred_element_type=F32
     )
     add_product(place, True)
+    pass_on(0)
     both("y0z")
     zs(0, -1)
     zs(0, 1)
@@ -236,6 +243,7 @@
     o_down2.start()
     y1z()
     y0x(1)
+    pass_on(1)
     turn(y, 0, BASIS)
     o_up[1].wait_recv()
     o_across_below = orb_copy(7, below, everything, partner)
@@ -243,12 +251,14 @@
     o_down[1].wait_recv()
     o_across_above = orb_copy(8, above, everything, partner)
     o_across_above.start()
+    pass_on(2)
     o_across.wait_recv()
     add_product(other(place))
     both("z0", -1)
     zs(1, -1)
     add_product(below)
     add_product(above)
+    pass_on(3)
     o_across_below.wait_recv()
     add_product(other(below))
     o_across_above.wait_recv()
@@ -261,6 +271,7 @@
     zs(1, 1)
     add_product(far)
     y0x(-1)
+    pass_on(4)
     o_across_far.wait_recv()
     add_product(other(far))
 
@@ -549,6 +560,7 @@
             dma((TERMS, TILES)),
             dma,
             dma,
+            pltpu.SemaphoreType.REGULAR((NZ // 2 + 1,)),
         ],
         compiler_params=pltpu.CompilerParams(
             collective_id=0, has_side_effects=True, vmem_limit_bytes=44 * 1024 * 1024

time: 71 us -> 68.2 us (0.961)
  Pallas kernels: 70.3 us -> 67.4 us
    pallas_call x1, Pallas kernels: 69.6 us -> 66.7 us  [on_device(): pl.pallas_call(kernel, out_shape=(jax.ShapeDtypeStruct((NY, WIN, COLS), B...]
where the time goes in v4:
time: 68.2 us; the launch traced here: 68.1 us
  Pallas kernels  67.4 us (99%)
    pallas_call x1, Pallas kernels, on_device(): pl.pallas_call(kernel, out_shape=(jax.ShapeDtypeStruct((NY, WIN, COLS), B...  66.7 us

profile of v4, /device:TPU:1, one launch (start us, length us, event | category | flops | bytes accessed | tf_op | source)
XLA Modules:
  0.0 68.1 jit_solution(14979538625763361778)
XLA Ops:
  0.6 66.7 %shard_map.77 = (bf16[4,112,256]{2,1,0:T(8,128)(2,1)S(1)}, f32[32,256]{1,0:T(8,128)S(1)}) custom-call(bf16[1,400,256]{2,1,0:T(8,128)(2,1)} %orb_in.1, bf16[1,400,400]{2,1,0:T(8,128)(2,1)} %inv_in.1, bf16[2048,512]{1,0:T(8,128)(2,1)} %interp_in.1, bf16[400,512]{1,0:T(8,128)(2,1)} %occ_in.1, bf16[512,256]{1,0:T(8,128)(2,1)} %chol_in.1, f32[32,256]{1,0:T(8,128)} %fields_in.1), custom_call_target="tpu_custom_call" | custom-call | tf_op jit(solution)/shard_map/pallas_call | solution.py:521
  67.4 0.7 %shard_map.78 = (bf16[1,400,256]{2,1,0:T(8,128)(2,1)}, f32[32,256]{1,0:T(8,128)}) custom-call(bf16[4,112,256]{2,1,0:T(8,128)(2,1)S(1)} %get-tuple-element.4.parts, f32[32,256]{1,0:T(8,128)S(1)} %get-tuple-element.5.bias_in), custom_call_target="tpu_custom_call" | custom-call | tf_op jit(solution)/shard_map/pallas_call | solution.py:574

commit v5 on v4

--- a/solution.py
+++ b/solution.py
@@ -16,10 +16,10 @@
 COLS = BASIS // CHOL
 WIN, STEP = 112, 96
 XROWS, XHALF = 192, 96
-ZROWS, ZHALF = 112, 64
+ZROWS, ZHALF = 96, 48
 ZBASE = NX * XROWS
 CBASE = ZBASE + NZ * ZROWS
-CROWS, CHALF = BASIS - CBASE, 192
+CROWS, CHALF = BASIS - CBASE, 256
 TILE = 512
 TILES = BASIS // TILE
 TURN = 512
@@ -275,17 +275,21 @@
     o_across_far.wait_recv()
     add_product(other(far))
 
+    def far_first(index):
+        away = lax.div(index + 1, 2) * (1 - 2 * lax.rem(index, 2))
+        return lax.rem(walk + WALK // 2 + away, WALK)
+
     weights[walk] = jnp.sum(gathered[...] * product[...], axis=0, keepdims=True)
 
-    def send_weights(step, carry):
+    def send_weights(index, carry):
         pltpu.make_async_remote_copy(
             src_ref=weights.at[walk], dst_ref=weights.at[walk],
             send_sem=small_send.at[0], recv_sem=small_recv.at[0],
-            device_id={"walk": lax.rem(walk + step, WALK), "chol": place}, device_id_type=MESH,
+            device_id={"walk": far_first(index), "chol": place}, device_id_type=MESH,
         ).start()
         return carry
 
-    lax.fori_loop(1, WALK, send_weights, 0)
+    lax.fori_loop(0, WALK - 1, send_weights, 0)
     both("y1z")
     zs(0, 2)
     both("y0x", 1)
@@ -306,10 +310,18 @@
         term[:, block * COLS : (block + 1) * COLS] = rows
         total[:, block * COLS : (block + 1) * COLS] = rows.astype(F32)
 
-    def multiply(block):
-        current[block] = dot(term[...], ip[block])
-
-    multiply(y)
+    def multiply(block, start, count, first=False):
+        rows = slice(start, start + count)
+        part = dot(term[:, rows], ip[block, rows, :])
+        current[block] = part if first else current[block] + part
+
+    x_rows, z_rows, c_rows = (0, ZBASE), (ZBASE, CBASE - ZBASE), (CBASE, CROWS)
+
+    def use(step, rows, first=False):
+        turn(at_y(step), *rows)
+        multiply(at_y(step), *rows, first)
+
+    multiply(y, 0, BASIS, True)
     some = weights.at[pl.ds(0, WALK - 1)]
     pltpu.make_async_copy(some, some, small_recv.at[0]).wait()
 
@@ -348,8 +360,8 @@
     part = sum_of_parts(dot_last(three_parts(coeff), chol[...]), WALK)
     field_part[...] = part.reshape(WALK, 1, PTS)
 
-    def send_scales(step, carry):
-        to = lax.rem(walk + step, WALK)
+    def send_scales(index, carry):
+        to = far_first(index)
         pltpu.make_async_remote_copy(
             src_ref=field_part.at[to], dst_ref=scale_in.at[walk],
             send_sem=small_send.at[2], recv_sem=small_recv.at[2],
@@ -357,7 +369,7 @@
         ).start()
         return carry
 
-    lax.fori_loop(1, WALK, send_scales, 0)
+    lax.fori_loop(0, WALK - 1, send_scales, 0)
     scale_in[walk] = field_part[walk]
     both("z1", 2)
     zs(2, 2)
@@ -373,13 +385,13 @@
     x1(2)
     both("z3", -1)
     both("z3", 1)
-    for step in (-1, 1):
-        turn(at_y(step), ZBASE, CBASE - ZBASE)
+    use(-1, z_rows, True)
+    use(1, z_rows, True)
     both("z2", 2)
     z3(2)
     both("y0c", -1)
-    for step in (-1, 1):
-        turn(at_y(step), CBASE, CROWS)
+    use(-1, c_rows)
+    use(1, c_rows)
     some_scales = scale_in.at[pl.ds(0, WALK - 1)]
     pltpu.make_async_copy(some_scales, some_scales, small_recv.at[2]).wait()
     scales[y] = jnp.sum(scale_in[...], axis=0)
@@ -396,15 +408,14 @@
 
     both("x1", -1)
     both("x1", 1)
-    for step in (-1, 1):
-        turn(at_y(step), 0, ZBASE)
-        multiply(at_y(step))
+    use(-1, x_rows)
+    use(1, x_rows)
     both("y1c")
+    use(2, c_rows, True)
+    both("x1", 2)
+    use(2, x_rows)
     both("z3", 2)
-    turn(at_y(2), ZBASE, BASIS - ZBASE)
-    both("x1", 2)
-    turn(at_y(2), 0, ZBASE)
-    multiply(at_y(2))
+    use(2, z_rows)
     some_blocks = scales.at[pl.ds(0, NY - 1)]
     pltpu.make_async_copy(some_blocks, some_blocks, small_recv.at[3]).wait()
 
@@ -423,10 +434,16 @@
 
     def points_to_basis(slot):
         mix(slot)
-        for tile in range(TILES):
-            columns = slice(tile * TILE, (tile + 1) * TILE)
-            own_part[slot, tile] = dot(mixed[...], turned[:, columns]).astype(BF16)
-            exchange(slot, tile).start()
+        for pair_of in range(0, TILES, 2):
+            columns = slice(pair_of * TILE, (pair_of + 2) * TILE)
+            value = dot(mixed[:, :PTS], turned[:PTS, columns])
+            for block in range(1, NY):
+                points = slice(block * PTS, (block + 1) * PTS)
+                value += dot(mixed[:, points], turned[points, columns])
+            for tile in (pair_of, pair_of + 1):
+                first = (tile - pair_of) * TILE
+                own_part[slot, tile] = value[:, first : first + TILE].astype(BF16)
+                exchange(slot, tile).start()
 
     def summed(slot, tile):
         exchange(slot, tile).wait_recv()

time: 68.2 us -> 67.4 us (0.988)
  Pallas kernels: 67.4 us -> 66.7 us
    pallas_call x1, Pallas kernels: 66.7 us -> 66 us  [on_device(): pl.pallas_call(kernel, out_shape=(jax.ShapeDtypeStruct((NY, WIN, COLS), B...]
where the time goes in v5:
time: 67.4 us; the launch traced here: 67.3 us
  Pallas kernels  66.7 us (99%)
    pallas_call x1, Pallas kernels, on_device(): pl.pallas_call(kernel, out_shape=(jax.ShapeDtypeStruct((NY, WIN, COLS), B...  66 us

profile of v5, /device:TPU:1, one launch (start us, length us, event | category | flops | bytes accessed | tf_op | source)
XLA Modules:
  0.0 67.3 jit_solution(10895979887100680109)
XLA Ops:
  0.6 66.0 %shard_map.77 = (bf16[4,112,256]{2,1,0:T(8,128)(2,1)S(1)}, f32[32,256]{1,0:T(8,128)S(1)}) custom-call(bf16[1,400,256]{2,1,0:T(8,128)(2,1)} %orb_in.1, bf16[1,400,400]{2,1,0:T(8,128)(2,1)} %inv_in.1, bf16[2048,512]{1,0:T(8,128)(2,1)} %interp_in.1, bf16[400,512]{1,0:T(8,128)(2,1)} %occ_in.1, bf16[512,256]{1,0:T(8,128)(2,1)} %chol_in.1, f32[32,256]{1,0:T(8,128)} %fields_in.1), custom_call_target="tpu_custom_call" | custom-call | tf_op jit(solution)/shard_map/pallas_call | solution.py:538
  66.6 0.7 %shard_map.78 = (bf16[1,400,256]{2,1,0:T(8,128)(2,1)}, f32[32,256]{1,0:T(8,128)}) custom-call(bf16[4,112,256]{2,1,0:T(8,128)(2,1)S(1)} %get-tuple-element.4.parts, f32[32,256]{1,0:T(8,128)S(1)} %get-tuple-element.5.bias_in), custom_call_target="tpu_custom_call" | custom-call | tf_op jit(solution)/shard_map/pallas_call | solution.py:591

commit v6 on v5

--- a/solution.py
+++ b/solution.py
@@ -454,10 +454,10 @@
 
     def one_term(slot, carry):
         points_to_basis(slot)
-        for tile in range(TILES):
-            value = summed(slot, tile)
+        for tile in range(0, TILES, 2):
+            value = jnp.concatenate([summed(slot, tile), summed(slot, tile + 1)], axis=1)
             for block in range(NY):
-                part = dot(value, ip[block, tile * TILE : (tile + 1) * TILE, :])
+                part = dot(value, ip[block, tile * TILE : (tile + 2) * TILE, :])
                 current[block] = current[block] + part if tile else part
         return carry
 

time: 67.4 us -> 67.8 us (level)
  no operation moved by 1% of the time
where the time goes in v6:
time: 67.8 us; the launch traced here: 67.7 us
  Pallas kernels  67.1 us (99%)
    pallas_call x1, Pallas kernels, on_device(): pl.pallas_call(kernel, out_shape=(jax.ShapeDtypeStruct((NY, WIN, COLS), B...  66.4 us

profile of v6, /device:TPU:1, one launch (start us, length us, event | category | flops | bytes accessed | tf_op | source)
XLA Modules:
  0.0 67.7 jit_solution(12807388231649649605)
XLA Ops:
  0.6 66.4 %shard_map.77 = (bf16[4,112,256]{2,1,0:T(8,128)(2,1)S(1)}, f32[32,256]{1,0:T(8,128)S(1)}) custom-call(bf16[1,400,256]{2,1,0:T(8,128)(2,1)} %orb_in.1, bf16[1,400,400]{2,1,0:T(8,128)(2,1)} %inv_in.1, bf16[2048,512]{1,0:T(8,128)(2,1)} %interp_in.1, bf16[400,512]{1,0:T(8,128)(2,1)} %occ_in.1, bf16[512,256]{1,0:T(8,128)(2,1)} %chol_in.1, f32[32,256]{1,0:T(8,128)} %fields_in.1), custom_call_target="tpu_custom_call" | custom-call | tf_op jit(solution)/shard_map/pallas_call | solution.py:538
  67.0 0.7 %shard_map.78 = (bf16[1,400,256]{2,1,0:T(8,128)(2,1)}, f32[32,256]{1,0:T(8,128)}) custom-call(bf16[4,112,256]{2,1,0:T(8,128)(2,1)S(1)} %get-tuple-element.4.parts, f32[32,256]{1,0:T(8,128)S(1)} %get-tuple-element.5.bias_in), custom_call_target="tpu_custom_call" | custom-call | tf_op jit(solution)/shard_map/pallas_call | solution.py:591
